TPU v7x, 32 devices: a whole 2x2x4 slice. The times are simulated.
32 devices in a mesh: band: 8 (over z, y), sub: 4 (over x, core).
Axes of the slice: x: 2, y: 2, z: 4, core: 2. Of those that a mesh axis runs over, the one named last changes fastest.
Arguments:
- grid_x: bfloat16 [227, 16384], P(None, ('band', 'sub')), may hold values from -6 to 6
- mesh_in: bfloat16 [2048, 512], P(('band', 'sub')), may hold values from -6 to 6
- w_embed: bfloat16 [227, 512], replicated, may hold values from -0.375 to 0.375
- w_src: bfloat16 [512, 512], replicated, may hold values from -0.25 to 0.25
- w_dst: bfloat16 [512, 512], replicated, may hold values from -0.25 to 0.25
- w_edge: bfloat16 [512, 512], replicated, may hold values from -0.25 to 0.25
- w_proc: bfloat16 [512, 512], replicated, may hold values from -0.25 to 0.25
- w_recv: bfloat16 [512, 512], replicated, may hold values from -0.25 to 0.25
- g2m_src: int32 [2048, 40], P(('band', 'sub')), may hold values from 0 to 16383, as said below
- mesh_src: int32 [2048, 6], P(('band', 'sub')), may hold values from 0 to 2047, as said below
- cotangent: bfloat16 [2048, 512], P(('band', 'sub')), may hold values from -6 to 6
Outputs:
- mesh_out: bfloat16 [2048, 512], P(('band', 'sub'))
- grid_grad: float32 [227, 16384], P(None, ('band', 'sub'))
- src_grad: float32 [512, 512], replicated
- edge_grad: float32 [512, 512], replicated
Inputs may be any that keep to these rules, and one draw needn't show every extreme that they name: Grid node g belongs to band g // (512 * 4), mesh node m to band m // (64 * 4); g2m_src[m, k] lies in the band of mesh node m, or among the 512 grid nodes of an adjacent band that stand next to that band in index order. mesh_src[m, j] lies in the band of mesh node m, or among the 64 mesh nodes of an adjacent band that stand next to that band in index order.
All inputs are finite; a program needn't handle non-finite values.
Results may differ from a plain program's by a relative error of at most 0.015.
Values may be sent and summed in bfloat16 or wider, within the bound.
A program may use at most 128 MiB of HBM per device.

v0:
```python
import functools
import math

import jax
import jax.numpy as jnp
from jax import lax
from jax.experimental import pallas as pl
from jax.experimental.pallas import tpu as pltpu
from jax.sharding import PartitionSpec as P

EPSILON = 1e-05
F32 = jnp.float32
BF16 = jnp.bfloat16
LANES = 128
INNER = 2
VMEM = pl.BlockSpec(memory_space=pltpu.VMEM)
SMEM = pl.BlockSpec(memory_space=pltpu.SMEM)
ANY = pl.BlockSpec(memory_space=pl.ANY)


def contract(left, right, left_dim, right_dim):
    return lax.dot_general(
        left, right, (((left_dim,), (right_dim,)), ((), ())), preferred_element_type=F32
    )


def silu_pair(value):
    sigma = 0.5 * jnp.tanh(0.5 * value) + 0.5
    active = value * sigma
    return active, sigma + active * (1.0 - sigma)


def remote(src, dst, send, recv, device):
    return pltpu.make_async_remote_copy(
        src_ref=src,
        dst_ref=dst,
        send_sem=send,
        recv_sem=recv,
        device_id=device,
        device_id_type=pl.DeviceIdType.MESH,
    )


def greet(barrier, device):
    pl.semaphore_signal(barrier, inc=1, device_id=device, device_id_type=pl.DeviceIdType.MESH)


class Place:
    def __init__(self, bands, subs):
        self.bands, self.subs = bands, subs
        self.band, self.me = lax.axis_index("band"), lax.axis_index("sub")
        self.core = lax.rem(self.me, 2)
        self.chip = self.me // 2
        self.partner = self.me + 1 - 2 * self.core
        self.chips = subs // 2
        self.outer, self.inner = self.band // INNER, lax.rem(self.band, INNER)
        self.outers = bands // INNER


def entry_barrier(at):
    barrier = pltpu.get_barrier_semaphore()
    for step in range(1, at.subs):
        greet(barrier, (at.band, lax.rem(at.me + step, at.subs)))

    @pl.when(at.band > 0)
    def _():
        for other in range(at.subs):
            greet(barrier, (at.band - 1, other))

    @pl.when(at.band < at.bands - 1)
    def _():
        for other in range(at.subs):
            greet(barrier, (at.band + 1, other))

    for i in range(1, at.outers):
        greet(barrier, (lax.rem(at.outer + i, at.outers) * INNER + at.inner, at.me))
    sides = jnp.minimum(at.band, 1) + jnp.minimum(at.bands - 1 - at.band, 1)
    pl.semaphore_wait(barrier, at.subs - 1 + at.subs * sides + at.outers - 1)


class Fetch:
    def __init__(self, at, src, o_ref, send, recv):
        self.at, self.src, self.o_ref, self.send, self.recv = at, src, o_ref, send, recv
        chips = at.chips
        self.across = [
            self.push(src, 1 + at.me, at.band, 2 * lax.rem(at.chip + k, chips) + at.core, k - 1)
            for k in range(1, chips)
        ]
        self.pair = self.push(src, 1 + at.me, at.band, at.partner, chips - 1)
        self.rising = (at.me == at.subs - 1) & (at.band < at.bands - 1)
        self.falling = (at.me == 0) & (at.band > 0)
        self.direct_below = (at.core == 1) & (at.band > 0)
        self.direct_above = (at.core == 0) & (at.band < at.bands - 1)
        top = at.subs + 1
        self.relay_below = self.push(o_ref.at[0], 0, at.band, at.partner, 4 * chips - 1)
        self.relay_above = self.push(o_ref.at[top], top, at.band, at.partner, 4 * chips)
        self.relays = []
        for k in range(1, chips):
            slot = self.near(k)
            self.relays.append(
                self.push(o_ref.at[slot], slot, at.band, at.partner, 3 * chips + k - 1)
            )

    def push(self, src, slot, b, s, index):
        return remote(src, self.o_ref.at[slot], self.send.at[index], self.recv.at[slot], (b, s))

    def near(self, k):
        at = self.at
        return 1 + 2 * lax.rem(at.chip + at.chips - k, at.chips) + at.core

    def up(self, k):
        at = self.at
        return self.push(self.src, 0, at.band + 1, 2 * k + 1, at.chips + k)

    def down(self, k):
        at = self.at
        return self.push(self.src, at.subs + 1, at.band - 1, 2 * k, 2 * at.chips + k)

    def arrived(self, slot):
        self.push(self.src, slot, self.at.band, self.at.partner, 0).wait_recv()

    def start(self):
        for copy in self.across:
            copy.start()
        self.pair.start()

        @pl.when(self.rising)
        def _():
            for k in range(self.at.chips):
                self.up(k).start()

        @pl.when(self.falling)
        def _():
            for k in range(self.at.chips):
                self.down(k).start()

    def clear(self):
        at = self.at
        block, kind = self.o_ref.shape[1:], self.o_ref.dtype

        @pl.when(at.band == 0)
        def _():
            self.o_ref[0] = jnp.zeros(block, kind)

        @pl.when(at.band == at.bands - 1)
        def _():
            self.o_ref[at.subs + 1] = jnp.zeros(block, kind)

    def wait_partner(self):
        self.arrived(1 + self.at.partner)

    def wait_near(self, k):
        self.arrived(self.near(k))
        self.relays[k - 1].start()

    def wait_far(self, k):
        self.arrived(self.near(k) + 1 - 2 * self.at.core)

    def wait_border(self):
        @pl.when(self.direct_below)
        def _():
            self.arrived(0)
            self.relay_below.start()

        @pl.when(self.direct_above)
        def _():
            self.arrived(self.at.subs + 1)
            self.relay_above.start()

    def wait_other_border(self):
        at = self.at

        @pl.when((at.core == 0) & (at.band > 0))
        def _():
            self.arrived(0)

        @pl.when((at.core == 1) & (at.band < at.bands - 1))
        def _():
            self.arrived(at.subs + 1)

    def finish(self):
        for copy in self.across + [self.pair] + self.relays:
            copy.wait_send()

        @pl.when(self.rising)
        def _():
            for k in range(self.at.chips):
                self.up(k).wait_send()

        @pl.when(self.falling)
        def _():
            for k in range(self.at.chips):
                self.down(k).wait_send()

        @pl.when(self.direct_below)
        def _():
            self.relay_below.wait_send()

        @pl.when(self.direct_above)
        def _():
            self.relay_above.wait_send()


def fetch_scratch(at_chips, subs):
    dma = pltpu.SemaphoreType.DMA
    return [dma((4 * at_chips + 1,)), dma((subs + 2,))]


class Return:
    def __init__(self, at, g_ref, pairbuf, stage, far, edge, send1, recv1, send2, far_sem, edge_sem):
        self.at, self.g_ref, self.pairbuf, self.stage = at, g_ref, pairbuf, stage
        self.far, self.edge, self.send2, self.edge_sem = far, edge, send2, edge_sem
        chips = at.chips
        self.swaps, self.across = {}, {}
        for step in range(chips + 1):
            self.swaps[step] = remote(
                g_ref.at[self.slot_of(step, 1 - at.core)],
                pairbuf.at[step],
                send1.at[step],
                recv1.at[step],
                (at.band, at.partner),
            )
        for step in range(1, chips):
            self.across[step] = remote(
                stage.at[step - 1],
                far.at[step - 1],
                send2.at[step - 1],
                far_sem.at[step - 1],
                (at.band, 2 * lax.rem(at.chip + step, chips) + at.core),
            )
        self.below = (at.core == 1) & (at.band > 0)
        self.above = (at.core == 0) & (at.band < at.bands - 1)

    def slot_of(self, step, which):
        at = self.at
        if step == at.chips:
            return (1 - which) * (at.subs + 1)
        return 1 + 2 * lax.rem(at.chip + step, at.chips) + which

    def border(self, b, s, chip):
        at = self.at
        last = at.chips - 1
        return remote(
            self.stage.at[last], self.edge.at[chip], self.send2.at[last], self.edge_sem.at[chip],
            (b, s),
        )

    def swap(self, step):
        self.swaps[step].start()

    def combined(self, step):
        self.swaps[step].wait_recv()
        mine = self.g_ref[self.slot_of(step, self.at.core)]
        return mine.astype(F32) + self.pairbuf[step].astype(F32)

    def send_across(self, step):
        self.stage[step - 1] = self.combined(step).astype(BF16)
        self.across[step].start()

    def send_border(self):
        at = self.at
        self.stage[at.chips - 1] = self.combined(at.chips).astype(BF16)

        @pl.when(self.below)
        def _():
            self.border(at.band - 1, at.subs - 1, at.chip).start()

        @pl.when(self.above)
        def _():
            self.border(at.band + 1, 0, at.chip).start()

    def total(self, o_ref):
        at = self.at
        total = self.combined(0)
        for step, copy in self.across.items():
            copy.wait_recv()
            total = total + self.far[step - 1].astype(F32)
        o_ref[...] = total

        def add_edges():
            extra = o_ref[...]
            for k in range(at.chips):
                self.border(at.band, at.partner, k).wait_recv()
                extra = extra + self.edge[k].astype(F32)
            o_ref[...] = extra

        @pl.when((at.me == at.subs - 1) & (at.band < at.bands - 1))
        def _():
            add_edges()

        @pl.when((at.me == 0) & (at.band > 0))
        def _():
            add_edges()

    def finish(self):
        at = self.at
        for copy in list(self.swaps.values()) + list(self.across.values()):
            copy.wait_send()

        @pl.when(self.below)
        def _():
            self.border(at.band - 1, at.subs - 1, at.chip).wait_send()

        @pl.when(self.above)
        def _():
            self.border(at.band + 1, 0, at.chip).wait_send()


def return_scratch(chips, block):
    dma = pltpu.SemaphoreType.DMA
    return [
        pltpu.VMEM((chips + 1,) + block, BF16),
        pltpu.VMEM((chips,) + block, BF16),
        pltpu.VMEM((chips,) + block, BF16),
        pltpu.VMEM((chips,) + block, BF16),
        dma((chips + 1,)),
        dma((chips + 1,)),
        dma((chips,)),
        dma((chips,)),
        dma((chips,)),
    ]


class Reduce:
    def __init__(self, at, v, o, r1, a1, r2, r3, s1, q1, s2, q2, s3, q3, s4, q4, s5, q5):
        self.at, self.v, self.o = at, v, o
        self.r1, self.a1, self.r2, self.r3 = r1, a1, r2, r3
        device = (at.band, at.partner)
        self.mine = at.chip * INNER + at.inner
        self.pair = remote(v.at[1 - at.core], r1, s1.at[0], q1.at[0], device)
        self.spread, self.back, self.relays = [], [], []
        own = o.at[at.core, self.mine]
        self.relays.append(remote(own, own, s5.at[0], q5.at[0], device))
        for dk in range(at.chips):
            for di in range(INNER):
                n = dk * INNER + di
                if n == 0:
                    continue
                chip, inner = lax.rem(at.chip + dk, at.chips), lax.rem(at.inner + di, INNER)
                goal = (at.outer * INNER + inner, 2 * chip + at.core)
                self.spread.append(
                    remote(a1.at[chip * INNER + inner], r2.at[n - 1], s2.at[n - 1], q2.at[n - 1], goal)
                )
                self.back.append(remote(own, own, s4.at[n - 1], q4.at[n - 1], goal))
                chip = lax.rem(at.chip + at.chips - dk, at.chips)
                inner = lax.rem(at.inner + INNER - di, INNER)
                part = o.at[at.core, chip * INNER + inner]
                self.relays.append(remote(part, part, s5.at[n], q5.at[n], device))
        self.exchange = []
        for i in range(1, at.outers):
            goal = (lax.rem(at.outer + i, at.outers) * INNER + at.inner, at.me)
            self.exchange.append(
                remote(r3.at[at.outer], r3.at[at.outer], s3.at[i - 1], q3.at[i - 1], goal)
            )

    def start(self):
        self.pair.start()

    def to_quarters(self):
        self.pair.wait_recv()
        self.a1[...] = (self.v[self.at.core].astype(F32) + self.r1[...].astype(F32)).astype(BF16)
        for copy in self.spread:
            copy.start()

    def to_exchange(self):
        total = self.a1[self.mine].astype(F32)
        for n, copy in enumerate(self.spread):
            copy.wait_recv()
            total = total + self.r2[n].astype(F32)
        self.r3[self.at.outer] = total.astype(BF16)
        for copy in self.exchange:
            copy.start()

    def to_back(self):
        for copy in self.exchange:
            copy.wait_recv()
        total = self.r3[0].astype(F32)
        for i in range(1, self.at.outers):
            total = total + self.r3[i].astype(F32)
        self.o[self.at.core, self.mine] = total.astype(BF16)
        for copy in self.back:
            copy.start()
        self.relays[0].start()

    def to_relay(self):
        for copy, relay in zip(self.back, self.relays[1:]):
            copy.wait_recv()
            relay.start()

    def finish(self):
        for copy in self.relays:
            copy.wait_recv()
        for copy in [self.pair] + self.spread + self.exchange + self.back + self.relays:
            copy.wait_send()


def reduce_shape(chips, rows, cols):
    quarters = chips * INNER
    return (2, quarters, rows // (2 * quarters), cols)


def reduce_scratch(chips, outers, rows, cols):
    dma = pltpu.SemaphoreType.DMA
    shape = reduce_shape(chips, rows, cols)
    quarters, piece = shape[1], shape[2:]
    return [
        pltpu.VMEM(shape[1:], BF16),
        pltpu.VMEM(shape[1:], BF16),
        pltpu.VMEM((quarters - 1,) + piece, BF16),
        pltpu.VMEM((outers,) + piece, BF16),
        dma((1,)),
        dma((1,)),
        dma((quarters - 1,)),
        dma((quarters - 1,)),
        dma((outers - 1,)),
        dma((outers - 1,)),
        dma((quarters - 1,)),
        dma((quarters - 1,)),
        dma((quarters,)),
        dma((quarters,)),
    ]


def take(refs, count):
    return refs[:count], refs[count:]


def whole_kernel(
    bands, subs, sizes,
    x_in, mesh_ref, we_in, ws_in, wd_in, wedge_in, wp_in, wr_in, gs_ref, gi_ref, mi_ref, cot_ref,
    mesh_out, grid_out, src_full, edge_full,
    xw, we, ws, wd, wedge, wp, wr, proj, rows_even, rows_odd, hid_t, slope_pre, dest,
    act, slope, normed, inverse, out_tile, encoded, hidden_mesh, receiver, picks,
    qwindow, mslope, rgrad, qslots, qgrad, mgrad, ugrad, grad, bgrad, edge_v,
    wgrad, left_v, right_v, gslots, src_out, edge_out, gv_ref, mv_ref, local,
    *rest,
):
    nodes, rows, enc, fan, latent, tile = sizes
    slots = subs + 2
    cols = latent // LANES
    half = latent // 2
    gathered = (rows_even, rows_odd)
    at = Place(bands, subs)
    fetch_x, rest = take(rest, 2)
    fetch_q, rest = take(rest, 2)
    return_q, rest = take(rest, 9)
    return_g, rest = take(rest, 9)
    scratch_e, rest = take(rest, 14)
    scratch_l, rest = take(rest, 14)
    scratch_r, rest = take(rest, 14)

    def load(src, dst, index):
        copy = pltpu.make_async_copy(src, dst, local.at[index])
        copy.start()
        return copy

    entry_barrier(at)
    xfetch = Fetch(at, x_in, xw, *fetch_x)
    xfetch.start()
    own_x = load(x_in, xw.at[1 + at.me], 0)
    loads = [
        load(src, dst, 1 + i)
        for i, (src, dst) in enumerate(
            [(we_in, we), (ws_in, ws), (wd_in, wd), (wedge_in, wedge), (wp_in, wp), (wr_in, wr)]
        )
    ]
    xfetch.clear()
    for k in range(enc):
        gv_ref[0:1, k * rows : (k + 1) * rows] = gi_ref[k : k + 1, :]
    for j in range(fan):
        mv_ref[0:1, j * rows : (j + 1) * rows] = mi_ref[j : j + 1, :]

    def embed(slot):
        for part in range(2):
            n = nodes // 2
            pre = contract(xw[slot, :, part * n : (part + 1) * n], we[...], 0, 0)
            active, slope_value = silu_pair(pre)
            active = active.astype(BF16)
            slope_pre[slot, part * n : (part + 1) * n] = slope_value.astype(BF16)
            column = pl.multiple_of(slot * nodes + part * n, n)
            hid_t[:, pl.ds(column, n)] = active.T
            value = jnp.dot(active, ws[...], preferred_element_type=F32)
            for j in range(cols):
                start = (slot * nodes + part * n) * cols + j
                proj[pl.ds(start, n, stride=cols), :] = value[:, j * LANES : (j + 1) * LANES]

    def step(i, carry):
        @pl.when(i == 1)
        def _():
            xfetch.wait_partner()

        for k in range(1, at.chips):
            @pl.when(i == 2 * k)
            def _(k=k):
                xfetch.wait_near(k)

            @pl.when(i == 2 * k + 1)
            def _(k=k):
                xfetch.wait_far(k)

        @pl.when(i == subs)
        def _():
            xfetch.wait_border()

        @pl.when(i == subs + 1)
        def _():
            xfetch.wait_other_border()

        odd = lax.rem(i, 2)
        side = at.core + odd - 2 * at.core * odd
        inside = 1 + 2 * lax.rem(at.chip + at.chips - i // 2 + at.chips, at.chips) + side
        outside = (1 - side) * (subs + 1)
        embed(jnp.where(i < subs, inside, outside))
        return carry

    for copy in loads[:3]:
        copy.wait()
    own_x.wait()
    dest[...] = jnp.dot(mesh_ref[...], wd[...], preferred_element_type=F32)
    lax.fori_loop(0, slots, step, 0)
    for copy in loads[3:]:
        copy.wait()

    chunk = tile * rows
    chunks = enc // tile
    first = at.band * (nodes * subs) - nodes
    encoded[...] = jnp.zeros_like(encoded)

    def gather(c, low, high):
        for r in range(low, high):
            k, m = divmod(c * chunk + r, rows)
            index = jnp.maximum(gs_ref[k, m] - first, 0) * cols
            gathered[c % 2][r * cols : (r + 1) * cols, :] = proj[pl.ds(index, cols), :]

    def before(c, t):
        base = (c * tile + t) * rows
        for j in range(cols):
            lane = slice(j * LANES, (j + 1) * LANES)
            value = gathered[c % 2][pl.ds(t * rows * cols + j, rows, stride=cols), :]
            active, slope_value = silu_pair(value + dest[:, lane])
            act[base : base + rows, lane] = active.astype(BF16)
            slope[base : base + rows, lane] = slope_value.astype(BF16)

    def norm(c, t):
        base = (c * tile + t) * rows
        out = out_tile[t * rows : (t + 1) * rows, :]
        out = out - jnp.mean(out, axis=-1, keepdims=True)
        factor = lax.rsqrt(jnp.mean(out * out, axis=-1, keepdims=True) + EPSILON)
        out = out * factor
        inverse[base : base + rows, :] = jnp.broadcast_to(factor, (rows, LANES))
        normed[base : base + rows, :] = out.astype(BF16)
        encoded[...] += out

    gather(0, 0, chunk)
    share = rows // 2
    for c in range(chunks):
        more = c + 1 < chunks
        for t in range(tile):
            if more:
                gather(c + 1, t * share, (t + 1) * share)
            before(c, t)
        out_tile[...] = jnp.dot(
            act[c * chunk : (c + 1) * chunk, :], wedge[...], preferred_element_type=F32
        )
        for t in range(tile):
            if more:
                gather(c + 1, (tile + t) * share, (tile + t + 1) * share)
            norm(c, t)

    mesh = mesh_ref[...].astype(F32) + encoded[...] * (1.0 / math.sqrt(enc))
    hidden_mesh[...] = mesh.astype(BF16)
    qwindow[1 + at.me] = jnp.dot(hidden_mesh[...], wp[...], preferred_element_type=F32).astype(BF16)
    qfetch = Fetch(at, qwindow.at[1 + at.me], qwindow, *fetch_q)
    qfetch.start()
    qfetch.clear()
    receiver[...] = jnp.dot(hidden_mesh[...], wr[...], preferred_element_type=F32)
    count = slots * rows
    mesh_first = at.band * (rows * subs) - rows
    node = lax.broadcasted_iota(jnp.int32, (count, fan * rows), 0)
    picks[...] = jnp.where(node == mv_ref[...] - mesh_first, 1.0, 0.0).astype(BF16)
    qfetch.wait_partner()
    for k in range(1, at.chips):
        qfetch.wait_near(k)
    qfetch.wait_border()
    for k in range(1, at.chips):
        qfetch.wait_far(k)
    qfetch.wait_other_border()
    mesh_before = contract(picks[...], qwindow[...].reshape(count, latent), 0, 0)
    upstream = cot_ref[...].astype(F32)
    scaled = upstream * (1.0 / math.sqrt(fan))
    summed = jnp.zeros((rows, latent), F32)
    received = jnp.zeros((rows, latent), F32)
    for j in range(fan):
        value = mesh_before[j * rows : (j + 1) * rows] + receiver[...]
        active, slope_value = silu_pair(value)
        summed = summed + active
        slope_value = scaled * slope_value
        received = received + slope_value
        mslope[j * rows : (j + 1) * rows] = slope_value.astype(BF16)
    window = jnp.dot(picks[...], mslope[...], preferred_element_type=F32)
    qslots[...] = window.astype(BF16).reshape(slots, rows, latent)
    qreturn = Return(at, qslots, *return_q)
    for s in list(range(1, at.chips)) + [at.chips, 0]:
        qreturn.swap(s)
    mesh_out[...] = (hidden_mesh[...].astype(F32) + summed * (1.0 / math.sqrt(fan))).astype(BF16)
    rgrad[...] = received.astype(BF16)
    for s in range(1, at.chips):
        qreturn.send_across(s)
    qreturn.send_border()
    mgrad[...] = upstream + contract(rgrad[...], wr[...], 1, 1)
    qreturn.total(qgrad)
    upper = mgrad[...] + contract(qgrad[...].astype(BF16), wp[...], 1, 1)
    upper = upper * (1.0 / math.sqrt(enc))
    mgrad[...] = upper
    ugrad[...] = upper - jnp.mean(upper, axis=-1, keepdims=True)

    def decode(k, carry):
        base = pl.multiple_of(k * rows, rows)
        value = normed[pl.ds(base, rows), :].astype(F32)
        both = jnp.mean(mgrad[...] * value, axis=-1, keepdims=True)
        out = (ugrad[...] - value * both) * inverse[pl.ds(base, rows), 0:1]
        grad[pl.ds(base, rows), :] = out.astype(BF16)
        return carry

    lax.fori_loop(0, enc, decode, 0, unroll=8)
    edge_value = contract(act[...], grad[...], 0, 0).astype(BF16)
    edge_v[...] = edge_value.reshape(edge_v.shape)
    edge = Reduce(at, edge_v, edge_out, *scratch_e)
    left = Reduce(at, left_v, src_out.at[:, :, :, 0:half], *scratch_l)
    right = Reduce(at, right_v, src_out.at[:, :, :, half:latent], *scratch_r)
    edge.start()
    back = contract(grad[...], wedge[...], 1, 1) * slope[...].astype(F32)
    bgrad[...] = back.astype(BF16)

    def scatter(h, slot):
        lane = slice(h * half, (h + 1) * half)
        node = lax.broadcasted_iota(jnp.int32, (nodes, enc * rows), 0) + (first + slot * nodes)
        hot = jnp.where(node == gv_ref[...], 1.0, 0.0).astype(BF16)
        total = jnp.dot(hot, bgrad[:, lane], preferred_element_type=F32)
        wgrad[pl.ds(pl.multiple_of(slot * nodes, nodes), nodes), lane] = total.astype(BF16)

    def source(h, ref):
        lane = slice(h * half, (h + 1) * half)
        total = jnp.dot(hid_t[...], wgrad[:, lane], preferred_element_type=F32)
        ref[...] = total.astype(BF16).reshape(ref.shape)

    def grid_back(slot):
        value = contract(wgrad[pl.ds(pl.multiple_of(slot * nodes, nodes), nodes), :], ws[...], 1, 1)
        value = (value * slope_pre[slot].astype(F32)).astype(BF16)
        gslots[slot] = contract(we[...], value, 1, 1).astype(BF16)

    greturn = Return(at, gslots, *return_g)

    def pair(s, work):
        def one(which, carry):
            if s == at.chips:
                slot = which * (subs + 1)
            else:
                slot = 1 + 2 * lax.rem(at.chip + s, at.chips) + which
            work(slot)
            return carry

        lax.fori_loop(0, 2, one, 0)

    def scatter_left(slot, carry):
        scatter(0, slot)
        return carry

    def scatter_right(slot):
        scatter(1, slot)

    edge.to_quarters()
    lax.fori_loop(0, slots, scatter_left, 0)
    edge.to_exchange()
    source(0, left_v)
    left.start()
    pair(at.chips, scatter_right)
    left.to_quarters()
    pair(at.chips, grid_back)
    greturn.swap(at.chips)
    for s in range(1, at.chips):
        pair(s, scatter_right)
    greturn.send_border()
    pair(0, scatter_right)
    left.to_exchange()
    source(1, right_v)
    right.start()
    for s in range(1, at.chips):
        pair(s, grid_back)
        greturn.swap(s)
    right.to_quarters()
    for s in range(1, at.chips):
        greturn.send_across(s)
    pair(0, grid_back)
    greturn.swap(0)
    right.to_exchange()
    edge.to_back()
    left.to_back()
    greturn.total(grid_out)
    right.to_back()
    edge.to_relay()
    left.to_relay()
    right.to_relay()
    for stream in (greturn, qreturn, xfetch, qfetch, edge, left):
        stream.finish()
    edge_full[...] = edge_out[...].astype(F32).reshape(latent, latent)
    src_full[:, 0:half] = src_out[:, :, :, 0:half].astype(F32).reshape(latent, half)
    right.finish()
    src_full[:, half:latent] = src_out[:, :, :, half:latent].astype(F32).reshape(latent, half)


def whole(bands, subs, sizes, channels, args):
    nodes, rows, enc, fan, latent, tile = sizes
    chips, outers, slots = subs // 2, bands // INNER, subs + 2
    edges = rows * enc
    half = latent // 2
    dma = pltpu.SemaphoreType.DMA
    square = pltpu.VMEM((latent, latent), BF16)
    small = pltpu.VMEM((rows, latent), F32)
    small_low = pltpu.VMEM((rows, latent), BF16)
    wide = pltpu.VMEM((edges, latent), BF16)
    scratch = [
        pltpu.VMEM((slots, channels, nodes), BF16),
        pltpu.VMEM((channels, latent), BF16),
        square, square, square, square, square,
        pltpu.VMEM((slots * nodes * latent // LANES, LANES), F32),
        pltpu.VMEM((tile * rows * latent // LANES, LANES), F32),
        pltpu.VMEM((tile * rows * latent // LANES, LANES), F32),
        pltpu.VMEM((latent, slots * nodes), BF16),
        pltpu.VMEM((slots, nodes, latent), BF16),
        small,
        wide, wide, wide,
        pltpu.VMEM((edges, LANES), F32),
        pltpu.VMEM((tile * rows, latent), F32),
        small, small_low, small,
        pltpu.VMEM((slots * rows, fan * rows), BF16),
        pltpu.VMEM((slots, rows, latent), BF16),
        pltpu.VMEM((fan * rows, latent), BF16),
        small_low,
        pltpu.VMEM((slots, rows, latent), BF16),
        small, small, small,
        wide, wide,
        pltpu.VMEM(reduce_shape(chips, latent, latent), BF16),
        pltpu.VMEM((slots * nodes, latent), BF16),
        pltpu.VMEM(reduce_shape(chips, latent, half), BF16),
        pltpu.VMEM(reduce_shape(chips, latent, half), BF16),
        pltpu.VMEM((slots, channels, nodes), BF16),
        pltpu.VMEM(reduce_shape(chips, latent, latent), BF16),
        pltpu.VMEM(reduce_shape(chips, latent, latent), BF16),
        pltpu.VMEM((1, edges), jnp.int32),
        pltpu.VMEM((1, fan * rows), jnp.int32),
        dma((7,)),
    ]
    scratch += fetch_scratch(chips, subs) * 2
    scratch += return_scratch(chips, (rows, latent)) + return_scratch(chips, (channels, nodes))
    scratch += reduce_scratch(chips, outers, latent, latent)
    scratch += reduce_scratch(chips, outers, latent, half) * 2
    return pl.pallas_call(
        functools.partial(whole_kernel, bands, subs, sizes),
        out_shape=[
            pltpu.VMEM((rows, latent), BF16),
            pltpu.VMEM((channels, nodes), F32),
            pltpu.VMEM((latent, latent), F32),
            pltpu.VMEM((latent, latent), F32),
        ],
        in_specs=[ANY, VMEM] + [ANY] * 6 + [SMEM, VMEM, VMEM, VMEM],
        out_specs=[VMEM] * 4,
        scratch_shapes=scratch,
        compiler_params=pltpu.CompilerParams(collective_id=0, has_side_effects=True, vmem_limit_bytes=60 << 20),
        name="whole",
    )(*args)


def finish_kernel(count, *refs):
    ins, outs, sems = refs[:count], refs[count : 2 * count], refs[2 * count]
    copies = [pltpu.make_async_copy(ins[i], outs[i], sems.at[i]) for i in range(count)]
    for copy in copies:
        copy.start()
    for copy in copies:
        copy.wait()


def finish(arrays):
    count = len(arrays)
    return pl.pallas_call(
        functools.partial(finish_kernel, count),
        out_shape=[jax.ShapeDtypeStruct(array.shape, array.dtype) for array in arrays],
        in_specs=[VMEM] * count,
        out_specs=[ANY] * count,
        scratch_shapes=[pltpu.SemaphoreType.DMA((count,))],
        compiler_params=pltpu.CompilerParams(vmem_limit_bytes=1 << 20),
        name="finish",
    )(*arrays)


def body(
    bands, subs,
    grid_x, mesh_in, w_embed, w_src, w_dst, w_edge, w_proc, w_recv, g2m_src, mesh_src, cotangent
):
    latent = w_src.shape[0]
    channels, nodes = grid_x.shape
    rows, enc = g2m_src.shape
    fan = mesh_src.shape[1]
    sizes = (nodes, rows, enc, fan, latent, 4)
    by_edge = g2m_src.T
    args = (
        grid_x, mesh_in, w_embed, w_src, w_dst, w_edge, w_proc, w_recv,
        by_edge, by_edge, mesh_src.T, cotangent,
    )
    return finish(whole(bands, subs, sizes, channels, args))


def solution(mesh):
    nodes = P(("band", "sub"), None)
    placed = (P(None, ("band", "sub")), nodes) + (P(),) * 6 + (nodes,) * 3
    return jax.shard_map(
        functools.partial(body, mesh.shape["band"], mesh.shape["sub"]),
        mesh=mesh,
        in_specs=placed,
        out_specs=(nodes, P(None, ("band", "sub")), P(), P()),
        check_vma=False,
    )
```

profile of v0, /device:TPU:0, one launch (start us, length us, event | category | flops | bytes accessed | tf_op | source)
XLA Modules:
  0.0 76.6 jit_solution(121403805504874446)
XLA Ops:
  0.6 74.2 %whole.1 = (bf16[64,512]{1,0:T(8,128)(2,1)S(1)}, f32[227,512]{1,0:T(8,128)S(1)}, f32[512,512]{1,0:T(8,128)S(1)}, f32[512,512]{1,0:T(8,128)S(1)}) custom-call(bf16[227,512]{1,0:T(8,128)(2,1)} %x_in.1, bf16[64,512]{1,0:T(8,128)(2,1)} %mesh_ref.1, bf16[227,512]{1,0:T(8,128)(2,1)} %we_in.1, bf16[512,512]{1,0:T(8,128)(2,1)} %ws_in.1, bf16[512,512]{1,0:T(8,128)(2,1)} %wd_in.1, ...), custom_call_target="tpu_custom_call" | custom-call | tf_op jit(solution)/shard_map/whole/pallas_call | solution.py:758
  74.9 1.5 %finish.1 = (bf16[64,512]{1,0:T(8,128)(2,1)}, f32[227,512]{1,0:T(8,128)}, f32[512,512]{1,0:T(8,128)}, f32[512,512]{1,0:T(8,128)}) custom-call(bf16[64,512]{1,0:T(8,128)(2,1)S(1)} %get-tuple-element.8.refs_0_, f32[227,512]{1,0:T(8,128)S(1)} %get-tuple-element.9.refs_1_, f32[512,512]{1,0:T(8,128)S(1)} %get-tuple-element.10.refs_2_, ...), custom_call_target="tpu_custom_call" | custom-call | tf_op jit(solution)/shard_map/finish/pallas_call | solution.py:785
where the time goes:
time: 76.9 us; the launch traced here: 76.6 us
  Pallas kernels  75.8 us (99%)
  between operations  0.8 us (1%)
    pallas_call x1, Pallas kernels, whole(): pl.pallas_call(functools.partial(whole_kernel, bands, subs, sizes), out_s...  74.2 us

commit v1 on v0

--- a/solution.py
+++ b/solution.py
@@ -484,7 +484,9 @@
                 start = (slot * nodes + part * n) * cols + j
                 proj[pl.ds(start, n, stride=cols), :] = value[:, j * LANES : (j + 1) * LANES]
 
-    def step(i, carry):
+    def step(turn, carry):
+        i = jnp.where(turn == subs - 1, subs, jnp.where(turn == subs, subs - 1, turn))
+
         @pl.when(i == 1)
         def _():
             xfetch.wait_partner()

time: 76.9 us -> 76.3 us (level)
  no operation moved by 1% of the time
where the time goes in v1:
time: 76.3 us; the launch traced here: 76.1 us
  Pallas kernels  75.3 us (99%)
  between operations  0.8 us (1%)
    pallas_call x1, Pallas kernels, whole(): pl.pallas_call(functools.partial(whole_kernel, bands, subs, sizes), out_s...  73.7 us
    pallas_call x1, Pallas kernels, finish(): pl.pallas_call(functools.partial(finish_kernel, count), out_shape=[jax.Sh...  1.53 us

profile of v1, /device:TPU:0, one launch (start us, length us, event | category | flops | bytes accessed | tf_op | source)
XLA Modules:
  0.0 76.1 jit_solution(18258109647390654530)
XLA Ops:
  0.6 73.7 %whole.1 = (bf16[64,512]{1,0:T(8,128)(2,1)S(1)}, f32[227,512]{1,0:T(8,128)S(1)}, f32[512,512]{1,0:T(8,128)S(1)}, f32[512,512]{1,0:T(8,128)S(1)}) custom-call(bf16[227,512]{1,0:T(8,128)(2,1)} %x_in.1, bf16[64,512]{1,0:T(8,128)(2,1)} %mesh_ref.1, bf16[227,512]{1,0:T(8,128)(2,1)} %we_in.1, bf16[512,512]{1,0:T(8,128)(2,1)} %ws_in.1, bf16[512,512]{1,0:T(8,128)(2,1)} %wd_in.1, ...), custom_call_target="tpu_custom_call" | custom-call | tf_op jit(solution)/shard_map/whole/pallas_call | solution.py:760
  74.4 1.5 %finish.1 = (bf16[64,512]{1,0:T(8,128)(2,1)}, f32[227,512]{1,0:T(8,128)}, f32[512,512]{1,0:T(8,128)}, f32[512,512]{1,0:T(8,128)}) custom-call(bf16[64,512]{1,0:T(8,128)(2,1)S(1)} %get-tuple-element.8.refs_0_, f32[227,512]{1,0:T(8,128)S(1)} %get-tuple-element.9.refs_1_, f32[512,512]{1,0:T(8,128)S(1)} %get-tuple-element.10.refs_2_, ...), custom_call_target="tpu_custom_call" | custom-call | tf_op jit(solution)/shard_map/finish/pallas_call | solution.py:787
